TPU v7x, 32 devices: a whole 2x2x4 slice. The times are simulated.
32 devices in a mesh: dp: 16 (over z, x, core), ctx: 2 (over y).
Axes of the slice: x: 2, y: 2, z: 4, core: 2. Of those that a mesh axis runs over, the one named last changes fastest.
Arguments:
- tokens: bfloat16 [16, 1024, 768], P('dp', 'ctx'), may hold values from -6 to 6
- block_table: int32 [4], replicated, may hold values from 0 to 3, as said below
- ln1_gain: bfloat16 [768], P('dp'), may hold values from 0.099609375 to 1.8984375
- ln1_bias: bfloat16 [768], P('dp'), may hold values from -3 to 3
- w_qkv: bfloat16 [768, 2304], P('dp'), may hold values from -0.21875 to 0.21875
- bias_query: bfloat16 [768], P('dp'), may hold values from -3 to 3
- bias_value: bfloat16 [768], P('dp'), may hold values from -3 to 3
- w_out: bfloat16 [768, 768], P('dp'), may hold values from -6 to 6
- bias_out: bfloat16 [768], P('dp'), may hold values from -3 to 3
- ln2_gain: bfloat16 [768], P('dp'), may hold values from 0.099609375 to 1.8984375
- ln2_bias: bfloat16 [768], P('dp'), may hold values from -3 to 3
- w_up: bfloat16 [768, 3072], P('dp'), may hold values from -0.21875 to 0.21875
- bias_up: bfloat16 [3072], P('dp'), may hold values from -3 to 3
- w_down: bfloat16 [3072, 768], P('dp'), may hold values from -0.109375 to 0.109375
- bias_down: bfloat16 [768], P('dp'), may hold values from -3 to 3
- cotangent: bfloat16 [16, 1024, 768], P('dp', 'ctx'), may hold values from -6 to 6
Outputs:
- output: bfloat16 [16, 1024, 768], P('dp', 'ctx')
- grad_tokens: bfloat16 [16, 1024, 768], P('dp', 'ctx')
- grad_ln1_gain: float32 [768], P('dp')
- grad_ln1_bias: float32 [768], P('dp')
- grad_w_qkv: float32 [768, 2304], P('dp')
- grad_bias_query: float32 [768], P('dp')
- grad_bias_value: float32 [768], P('dp')
- grad_w_out: float32 [768, 768], P('dp')
- grad_bias_out: float32 [768], P('dp')
- grad_ln2_gain: float32 [768], P('dp')
- grad_ln2_bias: float32 [768], P('dp')
- grad_w_up: float32 [768, 3072], P('dp')
- grad_bias_up: float32 [3072], P('dp')
- grad_w_down: float32 [3072, 768], P('dp')
- grad_bias_down: float32 [768], P('dp')
Inputs may be any that keep to these rules, and one draw needn't show every extreme that they name: block_table holds every block index of a sequence once; entries 2 i and 2 i + 1 are a mirrored pair b and 3 - b.
All inputs are finite; a program needn't handle non-finite values.
Results may differ from a plain program's by a relative error of at most 0.018.
Values may be sent and summed in bfloat16 or wider, within the bound.
A program may use at most 256 MiB of HBM per device.

v0:
```python
import jax
import jax.numpy as jnp
from jax import lax
from jax.sharding import PartitionSpec as P

HEADS = 12
HD = 64
BLK = 256


def layer_norm(values, gain, shift):
    centred = values - jnp.mean(values, axis=-1, keepdims=True)
    spread_sq = jnp.mean(centred * centred, axis=-1, keepdims=True)
    return centred * lax.rsqrt(spread_sq + 1e-05) * gain + shift


def gelu_tanh(values):
    return jax.nn.gelu(values, approximate=True)


def pair_scores(queries, keyvals, allowed, pair_index, model_width):
    pair_width = 2 * HD
    query_part = lax.dynamic_slice_in_dim(queries, pair_index * pair_width, pair_width, 1).reshape(
        queries.shape[0], 2, HD
    )
    key_part = lax.dynamic_slice_in_dim(keyvals, pair_index * pair_width, pair_width, 1).reshape(
        keyvals.shape[0], 2, HD
    )
    value_part = lax.dynamic_slice_in_dim(
        keyvals, model_width + pair_index * pair_width, pair_width, 1
    ).reshape(keyvals.shape[0], 2, HD)
    scores = jnp.einsum(
        "thd,shd->hts", query_part, key_part, preferred_element_type=jnp.float32
    ) * HD ** (-0.5)
    scores = jnp.where(allowed[None], scores, -1e30)
    return (query_part, key_part, value_part, scores)


def shards(
    tokens,
    block_table,
    ln1_gain,
    ln1_bias,
    w_qkv,
    bias_query,
    bias_value,
    w_out,
    bias_out,
    ln2_gain,
    ln2_bias,
    w_up,
    bias_up,
    w_down,
    bias_down,
    cotangent,
):
    model_width = tokens.shape[2]
    row_count = tokens.shape[1]
    key_count = row_count * lax.axis_size("ctx")
    pair_width = 2 * HD
    scale = HD ** (-0.5)
    fetched = (
        lax.all_gather(ln1_gain, "dp", axis=0, tiled=True),
        lax.all_gather(ln1_bias, "dp", axis=0, tiled=True),
        lax.all_gather(w_qkv, "dp", axis=0, tiled=True),
        lax.all_gather(bias_query, "dp", axis=0, tiled=True),
        lax.all_gather(bias_value, "dp", axis=0, tiled=True),
        lax.all_gather(w_out, "dp", axis=0, tiled=True),
        lax.all_gather(bias_out, "dp", axis=0, tiled=True),
        lax.all_gather(ln2_gain, "dp", axis=0, tiled=True),
        lax.all_gather(ln2_bias, "dp", axis=0, tiled=True),
        lax.all_gather(w_up, "dp", axis=0, tiled=True),
        lax.all_gather(bias_up, "dp", axis=0, tiled=True),
        lax.all_gather(w_down, "dp", axis=0, tiled=True),
        lax.all_gather(bias_down, "dp", axis=0, tiled=True),
    )
    (
        gain_one,
        shift_one,
        qkv_w,
        query_b,
        value_b,
        out_w,
        out_b,
        gain_two,
        shift_two,
        up_w,
        up_b,
        down_w,
        down_b,
    ) = fetched
    inputs = tokens[0].astype(jnp.float32)
    normed_one, norm_one_back = jax.vjp(
        layer_norm, inputs, gain_one.astype(jnp.float32), shift_one.astype(jnp.float32)
    )
    normed_one_low = normed_one.astype(jnp.bfloat16)
    bias_cat = jnp.concatenate(
        [
            query_b.astype(jnp.float32),
            jnp.zeros((model_width,), jnp.float32),
            value_b.astype(jnp.float32),
        ]
    )
    projected = (
        jnp.dot(normed_one_low, qkv_w, preferred_element_type=jnp.float32) + bias_cat
    ).astype(jnp.bfloat16)
    queries = projected[:, :model_width]
    own_keyvals = projected[:, model_width:]
    keyvals = lax.all_gather(own_keyvals, "ctx", axis=0, tiled=True)
    per_device = row_count // BLK
    owned_blocks = lax.dynamic_slice_in_dim(
        block_table, lax.axis_index("ctx") * per_device, per_device
    )
    query_block = jnp.repeat(owned_blocks, BLK, total_repeat_length=row_count)
    key_block = jnp.repeat(block_table, BLK, total_repeat_length=key_count)
    allowed = key_block[None, :] <= query_block[:, None]

    def forward_pair(pair_index, state_pair):
        attended_acc, log_sums = state_pair
        query_part, key_part, value_part, scores = pair_scores(
            queries, keyvals, allowed, pair_index, model_width
        )
        largest = jnp.max(scores, axis=-1, keepdims=True)
        exponent = jnp.exp(scores - largest)
        row_total = jnp.sum(exponent, axis=-1, keepdims=True)
        probs_low = (exponent / row_total).astype(jnp.bfloat16)
        mixed_pair = jnp.einsum(
            "hts,shd->thd", probs_low, value_part, preferred_element_type=jnp.float32
        )
        attended_acc = lax.dynamic_update_slice_in_dim(
            attended_acc, mixed_pair.reshape(row_count, pair_width), pair_index * pair_width, 1
        )
        log_sums = lax.dynamic_update_slice_in_dim(
            log_sums, (largest + jnp.log(row_total))[..., 0], pair_index * 2, 0
        )
        return (attended_acc, log_sums)

    attended, log_sums = lax.fori_loop(
        0,
        HEADS // 2,
        forward_pair,
        (
            jnp.zeros((row_count, model_width), jnp.float32),
            jnp.zeros((HEADS, row_count), jnp.float32),
        ),
    )
    attended_low = attended.astype(jnp.bfloat16)
    branch = jnp.dot(attended_low, out_w, preferred_element_type=jnp.float32) + out_b.astype(
        jnp.float32
    )
    middle = inputs + branch
    normed_two, norm_two_back = jax.vjp(
        layer_norm, middle, gain_two.astype(jnp.float32), shift_two.astype(jnp.float32)
    )
    normed_two_low = normed_two.astype(jnp.bfloat16)
    hidden_pre = jnp.dot(normed_two_low, up_w, preferred_element_type=jnp.float32) + up_b.astype(
        jnp.float32
    )
    active, gelu_back = jax.vjp(gelu_tanh, hidden_pre)
    active_low = active.astype(jnp.bfloat16)
    result = middle + (
        jnp.dot(active_low, down_w, preferred_element_type=jnp.float32) + down_b.astype(jnp.float32)
    )
    output = result.astype(jnp.bfloat16)[None]
    again_weights = (
        lax.all_gather(w_qkv, "dp", axis=0, tiled=True),
        lax.all_gather(w_out, "dp", axis=0, tiled=True),
        lax.all_gather(w_up, "dp", axis=0, tiled=True),
        lax.all_gather(w_down, "dp", axis=0, tiled=True),
    )
    qkv_back_w, out_back_w, up_back_w, down_back_w = again_weights
    upstream = cotangent[0]
    grad_down_w = jnp.einsum("tf,td->fd", active_low, upstream, preferred_element_type=jnp.float32)
    grad_down_b = jnp.sum(upstream.astype(jnp.float32), axis=0)
    grad_active = jnp.einsum("td,fd->tf", upstream, down_back_w, preferred_element_type=jnp.float32)
    grad_hidden = gelu_back(grad_active)[0].astype(jnp.bfloat16)
    grad_up_w = jnp.einsum(
        "td,tf->df", normed_two_low, grad_hidden, preferred_element_type=jnp.float32
    )
    grad_up_b = jnp.sum(grad_hidden.astype(jnp.float32), axis=0)
    grad_normed_two = jnp.einsum(
        "tf,df->td", grad_hidden, up_back_w, preferred_element_type=jnp.float32
    )
    grad_middle_norm, grad_gain_two, grad_shift_two = norm_two_back(grad_normed_two)
    grad_middle = upstream.astype(jnp.float32) + grad_middle_norm
    grad_branch = grad_middle.astype(jnp.bfloat16)
    grad_out_w = jnp.einsum(
        "td,te->de", attended_low, grad_branch, preferred_element_type=jnp.float32
    )
    grad_out_b = jnp.sum(grad_branch.astype(jnp.float32), axis=0)
    grad_attended = jnp.einsum(
        "te,de->td", grad_branch, out_back_w, preferred_element_type=jnp.float32
    ).astype(jnp.bfloat16)

    def backward_pair(pair_index, state_pair):
        grad_queries, grad_keyvals = state_pair
        query_part, key_part, value_part, scores = pair_scores(
            queries, keyvals, allowed, pair_index, model_width
        )
        log_part = lax.dynamic_slice_in_dim(log_sums, pair_index * 2, 2, 0)[:, :, None]
        probs = jnp.exp(scores - log_part)
        grad_part = lax.dynamic_slice_in_dim(
            grad_attended, pair_index * pair_width, pair_width, 1
        ).reshape(row_count, 2, HD)
        grad_probs = jnp.einsum(
            "thd,shd->hts", grad_part, value_part, preferred_element_type=jnp.float32
        )
        inner_sum = jnp.sum(probs * grad_probs, axis=-1, keepdims=True)
        grad_scores = (probs * (grad_probs - inner_sum) * scale).astype(jnp.bfloat16)
        grad_query = jnp.einsum(
            "hts,shd->thd", grad_scores, key_part, preferred_element_type=jnp.float32
        )
        grad_key = jnp.einsum(
            "hts,thd->shd", grad_scores, query_part, preferred_element_type=jnp.float32
        )
        grad_value = jnp.einsum(
            "hts,thd->shd",
            probs.astype(jnp.bfloat16),
            grad_part,
            preferred_element_type=jnp.float32,
        )
        grad_queries = lax.dynamic_update_slice_in_dim(
            grad_queries, grad_query.reshape(row_count, pair_width), pair_index * pair_width, 1
        )
        grad_keyvals = lax.dynamic_update_slice_in_dim(
            grad_keyvals, grad_key.reshape(key_count, pair_width), pair_index * pair_width, 1
        )
        grad_keyvals = lax.dynamic_update_slice_in_dim(
            grad_keyvals,
            grad_value.reshape(key_count, pair_width),
            model_width + pair_index * pair_width,
            1,
        )
        return (grad_queries, grad_keyvals)

    grad_queries, grad_keyvals = lax.fori_loop(
        0,
        HEADS // 2,
        backward_pair,
        (
            jnp.zeros((row_count, model_width), jnp.float32),
            jnp.zeros((key_count, 2 * model_width), jnp.float32),
        ),
    )
    grad_keyvals_own = lax.psum_scatter(
        grad_keyvals.astype(jnp.bfloat16), "ctx", scatter_dimension=0, tiled=True
    ).astype(jnp.float32)
    grad_projected = jnp.concatenate([grad_queries, grad_keyvals_own], axis=1).astype(jnp.bfloat16)
    grad_qkv_w = jnp.einsum(
        "td,te->de", normed_one_low, grad_projected, preferred_element_type=jnp.float32
    )
    column_sums = jnp.sum(grad_projected.astype(jnp.float32), axis=0)
    grad_query_b = column_sums[:model_width]
    grad_value_b = column_sums[2 * model_width :]
    grad_normed_one = jnp.einsum(
        "te,de->td", grad_projected, qkv_back_w, preferred_element_type=jnp.float32
    )
    grad_inputs_norm, grad_gain_one, grad_shift_one = norm_one_back(grad_normed_one)
    grad_tokens = (grad_middle + grad_inputs_norm).astype(jnp.bfloat16)[None]
    summed_rows = (
        lax.psum_scatter(
            grad_gain_one.astype(jnp.bfloat16), "dp", scatter_dimension=0, tiled=True
        ).astype(jnp.float32),
        lax.psum_scatter(
            grad_shift_one.astype(jnp.bfloat16), "dp", scatter_dimension=0, tiled=True
        ).astype(jnp.float32),
        lax.psum_scatter(
            grad_qkv_w.astype(jnp.bfloat16), "dp", scatter_dimension=0, tiled=True
        ).astype(jnp.float32),
        lax.psum_scatter(
            grad_query_b.astype(jnp.bfloat16), "dp", scatter_dimension=0, tiled=True
        ).astype(jnp.float32),
        lax.psum_scatter(
            grad_value_b.astype(jnp.bfloat16), "dp", scatter_dimension=0, tiled=True
        ).astype(jnp.float32),
        lax.psum_scatter(
            grad_out_w.astype(jnp.bfloat16), "dp", scatter_dimension=0, tiled=True
        ).astype(jnp.float32),
        lax.psum_scatter(
            grad_out_b.astype(jnp.bfloat16), "dp", scatter_dimension=0, tiled=True
        ).astype(jnp.float32),
        lax.psum_scatter(
            grad_gain_two.astype(jnp.bfloat16), "dp", scatter_dimension=0, tiled=True
        ).astype(jnp.float32),
        lax.psum_scatter(
            grad_shift_two.astype(jnp.bfloat16), "dp", scatter_dimension=0, tiled=True
        ).astype(jnp.float32),
        lax.psum_scatter(
            grad_up_w.astype(jnp.bfloat16), "dp", scatter_dimension=0, tiled=True
        ).astype(jnp.float32),
        lax.psum_scatter(
            grad_up_b.astype(jnp.bfloat16), "dp", scatter_dimension=0, tiled=True
        ).astype(jnp.float32),
        lax.psum_scatter(
            grad_down_w.astype(jnp.bfloat16), "dp", scatter_dimension=0, tiled=True
        ).astype(jnp.float32),
        lax.psum_scatter(
            grad_down_b.astype(jnp.bfloat16), "dp", scatter_dimension=0, tiled=True
        ).astype(jnp.float32),
    )
    (
        sum_gain_one,
        sum_shift_one,
        sum_qkv_w,
        sum_query_b,
        sum_value_b,
        sum_out_w,
        sum_out_b,
        sum_gain_two,
        sum_shift_two,
        sum_up_w,
        sum_up_b,
        sum_down_w,
        sum_down_b,
    ) = summed_rows
    final_grads = (
        lax.psum(sum_gain_one.astype(jnp.bfloat16), "ctx").astype(jnp.float32),
        lax.psum(sum_shift_one.astype(jnp.bfloat16), "ctx").astype(jnp.float32),
        lax.psum(sum_qkv_w.astype(jnp.bfloat16), "ctx").astype(jnp.float32),
        lax.psum(sum_query_b.astype(jnp.bfloat16), "ctx").astype(jnp.float32),
        lax.psum(sum_value_b.astype(jnp.bfloat16), "ctx").astype(jnp.float32),
        lax.psum(sum_out_w.astype(jnp.bfloat16), "ctx").astype(jnp.float32),
        lax.psum(sum_out_b.astype(jnp.bfloat16), "ctx").astype(jnp.float32),
        lax.psum(sum_gain_two.astype(jnp.bfloat16), "ctx").astype(jnp.float32),
        lax.psum(sum_shift_two.astype(jnp.bfloat16), "ctx").astype(jnp.float32),
        lax.psum(sum_up_w.astype(jnp.bfloat16), "ctx").astype(jnp.float32),
        lax.psum(sum_up_b.astype(jnp.bfloat16), "ctx").astype(jnp.float32),
        lax.psum(sum_down_w.astype(jnp.bfloat16), "ctx").astype(jnp.float32),
        lax.psum(sum_down_b.astype(jnp.bfloat16), "ctx").astype(jnp.float32),
    )
    return (
        output,
        grad_tokens,
        final_grads[0],
        final_grads[1],
        final_grads[2],
        final_grads[3],
        final_grads[4],
        final_grads[5],
        final_grads[6],
        final_grads[7],
        final_grads[8],
        final_grads[9],
        final_grads[10],
        final_grads[11],
        final_grads[12],
    )


def solution(mesh):
    in_specs = (
        P("dp", "ctx", None),
        P(),
        P("dp"),
        P("dp"),
        P("dp", None),
        P("dp"),
        P("dp"),
        P("dp", None),
        P("dp"),
        P("dp"),
        P("dp"),
        P("dp", None),
        P("dp"),
        P("dp", None),
        P("dp"),
        P("dp", "ctx", None),
    )
    out_specs = (
        P("dp", "ctx", None),
        P("dp", "ctx", None),
        P("dp"),
        P("dp"),
        P("dp", None),
        P("dp"),
        P("dp"),
        P("dp", None),
        P("dp"),
        P("dp"),
        P("dp"),
        P("dp", None),
        P("dp"),
        P("dp", None),
        P("dp"),
    )
    return jax.shard_map(shards, mesh=mesh, in_specs=in_specs, out_specs=out_specs, check_vma=False)
```

profile of v0, /device:TPU:0, one launch (start us, length us, event | category | flops | bytes accessed | tf_op | source)
XLA Modules:
  0.0 856.2 jit_solution(569629735728347137)
XLA Ops:
  17.3 63.3 %all-reduce.19 = (bf16[768]{0:T(1024)(128)(2,1)S(1)}, bf16[768]{0:T(1024)(128)(2,1)S(1)}, bf16[768]{0:T(1024)(128)(2,1)S(1)}, bf16[768]{0:T(1024)(128)(2,1)S(1)}...) all-reduce(bf16[768]{0:T(1024)(128)(2,1)S(1)} %dynamic-update-slice, ...), channel_id=1, replica_groups=mesh['dp'=16,'ctx'=2] {'dp'}, use_global_device_ids=true, to_apply=%add.4 | all-reduce | flops 8448 | bytes 33792
  97.2 34.6 %all-gather.8.cloned.1.call-done = bf16[1024,1536]{1,0:T(8,128)(2,1)} async-done(((bf16[512,1536]{1,0:T(8,128)(2,1)}), bf16[1024,1536]{1,0:T(8,128)(2,1)}) %all-gather.8.cloned.1.call-update) | async-done | bytes 3145744 | tf_op jit(solution)/shard_map/all_gather | solution.py:109
  136.6 57.0 %while.38 = (s32[]{:T(128)}, bf16[512,768]{0,1:T(8,128)(2,1)S(1)}, f32[12,512]{1,0:T(8,128)S(1)}, bf16[1024,1536]{0,1:T(8,128)(2,1)}, bf16[512,768]{0,1:T(8,128)...) while((s32[]{:T(128)}, bf16[512,768]{0,1:T(8,128)(2,1)S(1)}, ...), condition=%wide.region_5.6_spmd.clone, body=%wide.region_2.5_spmd.clone.sunk | while | flops 281541632 | bytes 33855824 | solution.py:138
  197.0 29.5 %all-gather.12.cloned.1.call-done = bf16[768,3072]{1,0:T(8,128)(2,1)} async-done(((bf16[48,3072]{1,0:T(8,128)(2,1)}), bf16[768,3072]{1,0:T(8,128)(2,1)}) %all-gather.12.cloned.1.call-update) | async-done | bytes 4718608 | tf_op jit(solution)/shard_map/all_gather | solution.py:72
  226.5 7.1 fusion.67
  233.6 46.7 %all-gather.14.cloned.1.call-done = bf16[3072,768]{1,0:T(8,128)(2,1)} async-done(((bf16[192,768]{1,0:T(8,128)(2,1)}), bf16[3072,768]{1,0:T(8,128)(2,1)}) %all-gather.14.cloned.1.call-update) | async-done | bytes 4718608 | tf_op jit(solution)/shard_map/all_gather | solution.py:74
  280.3 9.7 %fusion.77 = (bf16[3072]{0:T(1024)(128)(2,1)S(1)}, bf16[512,3072]{1,0:T(8,128)(2,1)S(1)}) fusion(f32[512,3072]{1,0:T(8,128)} %fusion.67, f32[3072]{0:T(1024)S(1)} %convert_element_type.214, bf16[3072,768]{1,0:T(8,128)(2,1)} %all-gather.14.cloned.1.call-done, bf16[1,512,768]{2,1,0:T(8,128)(2,1)S(1)} %copy-done.2), kind=kOutput, calls=%fused_computation.117 | convolution fusion | flops 2450519040 | bytes 14960640 | tf_op jit(solution)/shard_map/td,fd->tf/dot_general | solution.py:175
  301.1 171.1 %while.39 = (s32[]{:T(128)}, bf16[512,768]{0,1:T(8,128)(2,1)}, bf16[1024,1536]{0,1:T(8,128)(2,1)}, bf16[1024,1536]{0,1:T(8,128)(2,1)}, bf16[512,768]{0,1:T(8,128...) while((s32[]{:T(128)}, bf16[512,768]{0,1:T(8,128)(2,1)}, ...), condition=%wide.region_12.13_spmd.clone, body=%wide.region_10.12_spmd.clone.sunk | while | flops 686297088 | bytes 35539284 | solution.py:236
  310.6 7.1 fusion.141
  321.8 7.2 fusion.140
  339.1 7.1 fusion.141
  350.3 7.2 fusion.140
  367.6 7.1 fusion.141
  378.8 7.2 fusion.140
  396.1 7.1 fusion.141
  407.4 7.2 fusion.140
  424.7 7.1 fusion.141
  435.9 7.2 fusion.140
  453.2 7.1 fusion.141
  464.4 7.2 fusion.140
  476.6 8.1 convolution_convert_fusion.1
  485.8 8.6 %convolution_convert_fusion = bf16[3072,768]{1,0:T(8,128)(2,1)} fusion(bf16[1,512,768]{2,1,0:T(8,128)(2,1)S(1)} %copy-done.3, f32[512,3072]{1,0:T(8,128)} %fusion.67, f32[3072]{0:T(1024)S(1)} %convert_element_type.214), kind=kOutput, calls=%fused_computation.50 | convolution fusion | flops 2434007040 | bytes 11808768 | tf_op jit(solution)/shard_map/tf,td->fd/dot_general | solution.py:173
  494.4 20.0 %reduce-scatter.6.cloned.1.call-done = bf16[512,1536]{0,1:T(8,128)(2,1)} async-done(((bf16[1024,1536]{0,1:T(8,128)(2,1)}), bf16[512,1536]{0,1:T(8,128)(2,1)}) %reduce-scatter.6.cloned.1.call-update) | async-done | bytes 1572880 | tf_op jit(solution)/shard_map/reduce_scatter | solution.py:245
  514.4 5.7 convolution_convert_fusion.2
  524.1 5.1 fusion.68
  531.3 61.1 %all-reduce.18 = (bf16[768]{0:T(1024)(128)(2,1)S(1)}, bf16[768]{0:T(1024)(128)(2,1)S(1)}, bf16[768]{0:T(1024)(128)(2,1)S(1)}, bf16[768]{0:T(1024)(128)(2,1)S(1)}...) all-reduce(bf16[768]{0:T(1024)(128)(2,1)S(1)} %dynamic-update-slice, ...), channel_id=1, replica_groups=mesh['dp'=16,'ctx'=2] {'dp'}, use_global_device_ids=true, to_apply=%add.8 | all-reduce | flops 9984 | bytes 39936
  593.0 5.0 all-reduce.20
  605.6 49.1 %reduce-scatter.12.cloned.1.call-done = bf16[48,3072]{1,0:T(8,128)(2,1)} async-done(((bf16[768,3072]{1,0:T(8,128)(2,1)}), bf16[48,3072]{1,0:T(8,128)(2,1)}) %reduce-scatter.12.cloned.1.call-update) | async-done | bytes 294928 | tf_op jit(solution)/shard_map/reduce_scatter | solution.py:288
  654.8 78.8 %reduce-scatter.14.cloned.1.call-done = bf16[192,768]{1,0:T(8,128)(2,1)} async-done(((bf16[3072,768]{1,0:T(8,128)(2,1)}), bf16[192,768]{1,0:T(8,128)(2,1)}) %reduce-scatter.14.cloned.1.call-update) | async-done | bytes 294928 | tf_op jit(solution)/shard_map/reduce_scatter | solution.py:294
  733.5 71.1 %reduce-scatter.8.cloned.1.call-done = bf16[48,2304]{1,0:T(8,128)(2,1)} async-done(((bf16[768,2304]{1,0:T(8,128)(2,1)}), bf16[48,2304]{1,0:T(8,128)(2,1)}) %reduce-scatter.8.cloned.1.call-update) | async-done | bytes 221200 | tf_op jit(solution)/shard_map/reduce_scatter | solution.py:267
  804.6 9.5 %fusion.48 = bf16[1,512,768]{2,1,0:T(8,128)(2,1)} fusion(f32[512,768]{1,0:T(8,128)} %copy-done.4, bf16[3072,768]{1,0:T(8,128)(2,1)} %all-gather.14.cloned.1.call-done, f32[768]{0:T(1024)S(1)} %convert_element_type.216, f32[512,3072]{1,0:T(8,128)} %fusion.67, f32[3072]{0:T(1024)S(1)} %convert_element_type.214), kind=kOutput, calls=%fused_computation.82 | convolution fusion | flops 2432827392 | bytes 13384704 | tf_op jit(solution)/shard_map/dot_general | solution.py:162
  814.1 28.5 %all-reduce.24.cloned.1.call-done = (bf16[48,2304]{1,0:T(8,128)(2,1)}, bf16[48,768]{1,0:T(8,128)(2,1)}, bf16[48,3072]{1,0:T(8,128)(2,1)}, bf16[192,768]{1,0:T(8,128)(2,1)}) async-done(((bf16[48,2304]{1,0:T(8,128)(2,1)}, bf16[48,768]{1,0:T(8,128)(2,1)}, bf16[48,3072]{1,0:T(8,128)(2,1)}, bf16[192,768]{1,0:T(8,128)(2,1)}), (bf16[48,2304]{1,0:T(8,128)(2,1)}, bf16[48,768]{1,0:T(8,128)(2,1)}, ...) | async-done | bytes 884752 | tf_op jit(solution)/shard_map/psum | solution.py:319
  (281 shorter events, 211.3 us)
Async XLA Ops:
  7.2 76.3 %all-gather.6.cloned.1.call-start = ((), (), s32[]{:S(2)}) async-start(), calls=%async_computation.5 | async-start | bytes 3760128 | tf_op jit(solution)/shard_map/all_gather | solution.py:65
  7.9 123.8 %all-gather.8.cloned.1.call-start = ((), (), s32[]{:S(2)}) async-start(), calls=%async_computation.6 | async-start | bytes 4718592 | tf_op jit(solution)/shard_map/all_gather | solution.py:109
  87.9 3.6 copy-start.10
  87.9 4.9 copy-start.14
  88.0 6.2 copy-start.11
  88.0 6.2 copy-start.12
  88.0 6.2 copy-start.13
  89.3 104.3 %all-gather.10.cloned.1.call-start = ((), (), s32[]{:S(2)}) async-start(), calls=%async_computation.7 | async-start | bytes 1253376 | tf_op jit(solution)/shard_map/all_gather | solution.py:68
  90.0 136.4 %all-gather.12.cloned.1.call-start = ((), (), s32[]{:S(2)}) async-start(), calls=%async_computation.8 | async-start | bytes 5013504 | tf_op jit(solution)/shard_map/all_gather | solution.py:72
  90.6 189.7 %all-gather.14.cloned.1.call-start = ((), (), s32[]{:S(2)}) async-start(), calls=%async_computation.9 | async-start | bytes 5013504 | tf_op jit(solution)/shard_map/all_gather | solution.py:74
  91.2 423.2 %reduce-scatter.6.cloned.1.call-start = ((), (), s32[]{:S(2)}) async-start(), calls=%async_computation.10 | async-start | bytes 4718592 | tf_op jit(solution)/shard_map/reduce_scatter | solution.py:245
  136.6 57.9 %copy-start.1 = (bf16[1,512,768]{2,1,0:T(8,128)(2,1)S(1)}, bf16[1,512,768]{2,1,0:T(8,128)(2,1)}, u32[]{:S(2)}) copy-start(bf16[1,512,768]{2,1,0:T(8,128)(2,1)} %param.24) | copy-start | bytes 2359300
  139.2 2.0 copy-start
  148.7 2.0 copy-start
  158.1 2.0 copy-start
  167.6 2.0 copy-start
  177.1 2.0 copy-start
  186.7 2.0 copy-start
  193.6 3.4 copy-start.7
  196.7 93.3 %copy-start.4 = (f32[512,768]{1,0:T(8,128)}, f32[512,768]{1,0:T(8,128)S(1)}, u32[]{:S(2)}) copy-start(f32[512,768]{1,0:T(8,128)S(1)} %get-tuple-element.560) | copy-start | bytes 4718596
  197.0 83.3 %copy-start.2 = (bf16[1,512,768]{2,1,0:T(8,128)(2,1)S(1)}, bf16[1,512,768]{2,1,0:T(8,128)(2,1)}, u32[]{:S(2)}) copy-start(bf16[1,512,768]{2,1,0:T(8,128)(2,1)} %param.39) | copy-start | bytes 2359300
  280.3 9.7 %copy-start.15 = (bf16[768,3072]{1,0:T(8,128)(2,1)S(1)}, bf16[768,3072]{1,0:T(8,128)(2,1)}, u32[]{:S(2)}) copy-start(bf16[768,3072]{1,0:T(8,128)(2,1)} %all-gather.12.cloned.1.call-done) | copy-start | bytes 14155780
  290.0 3.0 copy-start.18
  293.0 3.3 copy-start.16
  472.2 1.1 copy-start.8
  472.3 133.4 %reduce-scatter.10.cloned.1.call-start = ((), (), s32[]{:S(2)}) async-start(), calls=%async_computation.12 | async-start | bytes 1253376 | tf_op jit(solution)/shard_map/reduce_scatter | solution.py:276
  476.3 178.4 %reduce-scatter.12.cloned.1.call-start = ((), (), s32[]{:S(2)}) async-start(), calls=%async_computation.13 | async-start | bytes 5013504 | tf_op jit(solution)/shard_map/reduce_scatter | solution.py:288
  484.7 248.9 %reduce-scatter.14.cloned.1.call-start = ((), (), s32[]{:S(2)}) async-start(), calls=%async_computation.14 | async-start | bytes 5013504 | tf_op jit(solution)/shard_map/reduce_scatter | solution.py:294
  494.4 310.2 %reduce-scatter.8.cloned.1.call-start = ((), (), s32[]{:S(2)}) async-start(), calls=%async_computation.11 | async-start | bytes 3760128 | tf_op jit(solution)/shard_map/reduce_scatter | solution.py:267
  520.1 1.8 copy-start.17
  520.1 322.4 %all-reduce.24.cloned.1.call-start = ((), (), s32[]{:S(2)}) async-start(), calls=%async_computation.15 | async-start | bytes 1769472 | tf_op jit(solution)/shard_map/psum | solution.py:319
  529.3 1.2 copy-start.5
  (3 other events, 2.9 us)
Sparse Core Ops, SparseCore 0:
  10.3 50.2 all-gather.5
  89.4 42.2 all-gather.7
  134.0 38.2 all-gather.9
  174.5 51.9 all-gather.11
  228.6 51.6 all-gather.13
  472.4 41.9 reduce-scatter.5
  518.0 58.1 reduce-scatter.9
  580.1 74.6 reduce-scatter.11
  658.6 74.8 reduce-scatter.13
  737.3 67.3 reduce-scatter.7
  807.1 35.3 all-reduce.23
where the time goes:
time: 862 us; the launch traced here: 856 us
  waiting for transfers between devices  361 us (42%)
  matrix products  234 us (27%)
  blocking collectives  129 us (15%)
  local copies, waits for them, and re-layouts  74.3 us (9%)
  other arithmetic  38.5 us (4%)
  between operations  17.1 us (2%)
    unnamed x2, blocking collectives  124 us
    reduce_scatter x1, waiting for transfers between devices, shards(): lax.psum_scatter(grad_down_w.astype(jnp.bfloat16), 'dp', scatter_dimensio...  78.8 us
    reduce_scatter x1, waiting for transfers between devices, shards(): lax.psum_scatter(grad_qkv_w.astype(jnp.bfloat16), 'dp', scatter_dimension...  71.1 us
    reduce_scatter x1, waiting for transfers between devices, shards(): lax.psum_scatter(grad_up_w.astype(jnp.bfloat16), 'dp', scatter_dimension=...  49.1 us
    all_gather x1, waiting for transfers between devices, shards(): lax.all_gather(w_down, 'dp', axis=0, tiled=True)  46.7 us
    dot_general x6, matrix products, backward_pair(): jnp.einsum('hts,shd->thd', grad_scores, key_part, preferred_element_type=...  43.1 us
    dot_general x6, matrix products, backward_pair(): jnp.einsum('hts,thd->shd', grad_scores, query_part, preferred_element_typ...  42.6 us
    all_gather x1, waiting for transfers between devices, shards(): keyvals = lax.all_gather(own_keyvals, 'ctx', axis=0, tiled=True)  34.6 us
  transfers between devices with their start and end apart: 11, of which 8 were waited for; matrix products, arithmetic and copies ran while one was open for 15% of the time, Pallas kernels for 0%

commit v1 on v0

--- a/solution.py
+++ b/solution.py
@@ -316,7 +316,7 @@
     final_grads = (
         lax.psum(sum_gain_one.astype(jnp.bfloat16), "ctx").astype(jnp.float32),
         lax.psum(sum_shift_one.astype(jnp.bfloat16), "ctx").astype(jnp.float32),
-        lax.psum(sum_qkv_w.astype(jnp.bfloat16), "ctx").astype(jnp.float32),
+        jnp.sum(lax.all_gather(sum_qkv_w.astype(jnp.bfloat16), "ctx"), axis=0).astype(jnp.float32),
         lax.psum(sum_query_b.astype(jnp.bfloat16), "ctx").astype(jnp.float32),
         lax.psum(sum_value_b.astype(jnp.bfloat16), "ctx").astype(jnp.float32),
         lax.psum(sum_out_w.astype(jnp.bfloat16), "ctx").astype(jnp.float32),

time: 862 us -> 684 us (0.79)
  waiting for transfers between devices: 361 us -> 176 us
    reduce_scatter x1, waiting for transfers between devices: 71.1 us -> 0.01 us  [shards(): lax.psum_scatter(grad_qkv_w.astype(jnp.bfloat16), 'dp', scatter_dimension...]
    reduce_scatter x1, waiting for transfers between devices: 78.8 us -> 17 us  [shards(): lax.psum_scatter(grad_down_w.astype(jnp.bfloat16), 'dp', scatter_dimensio...]
    reduce_scatter x1, waiting for transfers between devices: 49.1 us -> 0.02 us  [shards(): lax.psum_scatter(grad_up_w.astype(jnp.bfloat16), 'dp', scatter_dimension=...]
    psum x1, waiting for transfers between devices: 28.5 us -> 0.01 us  [shards(): lax.psum(sum_out_w.astype(jnp.bfloat16), 'ctx').astype(jnp.float32)]
    reduce_scatter x1, waiting for transfers between devices: 20 us -> 44.9 us  [shards(): lax.psum_scatter(grad_keyvals.astype(jnp.bfloat16), 'ctx', scatter_dimens...]
    unnamed x66 -> x74, local copies, waits for them, and re-layouts: 19 us -> 19 us
  transfers between devices with their start and end apart: 11 -> 11, of which waited for: 8 -> 5; matrix products, arithmetic and copies ran while one was open for 15% -> 45% of each run, Pallas kernels for 0% -> 0%
where the time goes in v1:
time: 684 us; the launch traced here: 678 us
  matrix products  235 us (34%)
  waiting for transfers between devices  176 us (26%)
  blocking collectives  137 us (20%)
  local copies, waits for them, and re-layouts  73.8 us (11%)
  other arithmetic  37.6 us (5%)
  between operations  17.2 us (3%)
    unnamed x2, blocking collectives  125 us
    all_gather x1, waiting for transfers between devices, shards(): lax.all_gather(w_down, 'dp', axis=0, tiled=True)  46.8 us
    reduce_scatter x1, waiting for transfers between devices, shards(): lax.psum_scatter(grad_keyvals.astype(jnp.bfloat16), 'ctx', scatter_dimens...  44.9 us
    dot_general x6, matrix products, backward_pair(): jnp.einsum('hts,shd->thd', grad_scores, key_part, preferred_element_type=...  44 us
    dot_general x6, matrix products, backward_pair(): jnp.einsum('hts,thd->shd', grad_scores, query_part, preferred_element_typ...  43.5 us
    all_gather x1, waiting for transfers between devices, shards(): keyvals = lax.all_gather(own_keyvals, 'ctx', axis=0, tiled=True)  34.4 us
    all_gather x1, waiting for transfers between devices, shards(): lax.all_gather(w_up, 'dp', axis=0, tiled=True)  30.2 us
    dot_general x12, matrix products, pair_scores(): jnp.einsum('thd,shd->hts', query_part, key_part, preferred_element_type=j...  25.7 us
  transfers between devices with their start and end apart: 11, of which 5 were waited for; matrix products, arithmetic and copies ran while one was open for 45% of the time, Pallas kernels for 0%

profile of v1, /device:TPU:0, one launch (start us, length us, event | category | flops | bytes accessed | tf_op | source)
XLA Modules:
  0.0 678.1 jit_solution(5542650432229149000)
XLA Ops:
  17.3 63.3 %all-reduce.19 = (bf16[768]{0:T(1024)(128)(2,1)S(1)}, bf16[768]{0:T(1024)(128)(2,1)S(1)}, bf16[768]{0:T(1024)(128)(2,1)S(1)}, bf16[768]{0:T(1024)(128)(2,1)S(1)}...) all-reduce(bf16[768]{0:T(1024)(128)(2,1)S(1)} %dynamic-update-slice, ...), channel_id=1, replica_groups=mesh['dp'=16,'ctx'=2] {'dp'}, use_global_device_ids=true, to_apply=%add.4 | all-reduce | flops 8448 | bytes 33792
  83.5 4.4 fusion.34
  97.4 34.4 %all-gather.9.cloned.1.call-done = bf16[1024,1536]{1,0:T(8,128)(2,1)} async-done(((bf16[512,1536]{1,0:T(8,128)(2,1)}), bf16[1024,1536]{1,0:T(8,128)(2,1)}) %all-gather.9.cloned.1.call-update) | async-done | bytes 3145744 | tf_op jit(solution)/shard_map/all_gather | solution.py:109
  131.7 4.6 copy.36
  136.5 56.4 %while.38 = (s32[]{:T(128)}, bf16[512,768]{0,1:T(8,128)(2,1)S(1)}, f32[12,512]{1,0:T(8,128)S(1)}, bf16[1024,1536]{0,1:T(8,128)(2,1)}, bf16[512,768]{0,1:T(8,128)...) while((s32[]{:T(128)}, bf16[512,768]{0,1:T(8,128)(2,1)S(1)}, ...), condition=%wide.region_5.6_spmd.clone, body=%wide.region_2.5_spmd.clone.sunk | while | flops 281541632 | bytes 33855824 | solution.py:138
  196.3 30.2 %all-gather.13.cloned.1.call-done = bf16[768,3072]{1,0:T(8,128)(2,1)} async-done(((bf16[48,3072]{1,0:T(8,128)(2,1)}), bf16[768,3072]{1,0:T(8,128)(2,1)}) %all-gather.13.cloned.1.call-update) | async-done | bytes 4718608 | tf_op jit(solution)/shard_map/all_gather | solution.py:72
  226.5 7.1 %fusion.67 = f32[512,3072]{1,0:T(8,128)} fusion(bf16[768,3072]{1,0:T(8,128)(2,1)} %all-gather.13.cloned.1.call-done, f32[512,768]{1,0:T(8,128)S(1)} %get-tuple-element.559, f32[768]{0:T(1024)S(1)} %convert_element_type.214, f32[768]{0:T(1024)S(1)} %convert_element_type.213, f32[512]{0:T(512)S(1)} %fusion.61, f32[512]{0:T(512)S(1)} %broadcast_multiply_fusion), kind=kOutput, calls=%fused_computation.108 | convolution fusion | flops 2417885184 | bytes 12593152 | tf_op jit(solution)/shard_map/dot_general | solution.py:156
  233.6 46.8 %all-gather.15.cloned.1.call-done = bf16[3072,768]{1,0:T(8,128)(2,1)} async-done(((bf16[192,768]{1,0:T(8,128)(2,1)}), bf16[3072,768]{1,0:T(8,128)(2,1)}) %all-gather.15.cloned.1.call-update) | async-done | bytes 4718608 | tf_op jit(solution)/shard_map/all_gather | solution.py:74
  280.4 9.3 %fusion.77 = (bf16[3072]{0:T(1024)(128)(2,1)S(1)}, bf16[512,3072]{1,0:T(8,128)(2,1)S(1)}) fusion(f32[512,3072]{1,0:T(8,128)} %fusion.67, f32[3072]{0:T(1024)S(1)} %convert_element_type.216, bf16[3072,768]{1,0:T(8,128)(2,1)} %all-gather.15.cloned.1.call-done, bf16[1,512,768]{2,1,0:T(8,128)(2,1)S(1)} %copy-done.2), kind=kOutput, calls=%fused_computation.117 | convolution fusion | flops 2450519040 | bytes 14960640 | tf_op jit(solution)/shard_map/td,fd->tf/dot_general | solution.py:175
  297.9 7.5 %convolution_convert_fusion.1 = bf16[768,3072]{1,0:T(8,128)(2,1)} fusion(bf16[512,3072]{1,0:T(8,128)(2,1)} %copy-done.22, f32[512,768]{1,0:T(8,128)} %copy-done.4, f32[768]{0:T(1024)S(1)} %convert_element_type.214, f32[768]{0:T(1024)S(1)} %convert_element_type.213, f32[512]{0:T(512)S(1)} %fusion.61, f32[512]{0:T(512)S(1)} %broadcast_multiply_fusion), kind=kOutput, calls=%fused_computation.51 | convolution fusion | flops 2420244480 | bytes 9447424 | tf_op jit(solution)/shard_map/td,tf->df/dot_general | solution.py:177
  305.4 8.7 %convolution_convert_fusion = bf16[3072,768]{1,0:T(8,128)(2,1)} fusion(bf16[1,512,768]{2,1,0:T(8,128)(2,1)S(1)} %copy-done.2, f32[512,3072]{1,0:T(8,128)} %fusion.67, f32[3072]{0:T(1024)S(1)} %convert_element_type.216), kind=kOutput, calls=%fused_computation.50 | convolution fusion | flops 2434007040 | bytes 11808768 | tf_op jit(solution)/shard_map/tf,td->fd/dot_general | solution.py:173
  321.3 173.5 %while.39 = (s32[]{:T(128)}, bf16[512,768]{0,1:T(8,128)(2,1)}, bf16[1024,1536]{0,1:T(8,128)(2,1)}, bf16[1024,1536]{0,1:T(8,128)(2,1)}, bf16[512,768]{0,1:T(8,128...) while((s32[]{:T(128)}, bf16[512,768]{0,1:T(8,128)(2,1)}, ...), condition=%wide.region_12.13_spmd.clone, body=%wide.region_10.12_spmd.clone.sunk | while | flops 686297088 | bytes 35539284 | solution.py:236
  330.9 7.1 %fusion.141 = bf16[2,64,1024]{2,1,0:T(8,128)(2,1)S(1)} fusion(bf16[512,2,64]{0,2,1:T(8,128)(2,1)S(1)} %bitcast.157, f32[2,512,1024]{2,1,0:T(8,128)} %subtract_exponential_fusion.3, f32[2,512,1024]{2,1,0:T(8,128)} %fusion.139), kind=kOutput, calls=%fused_computation.21.clone.1 | convolution fusion | flops 139462656 | bytes 8781824 | tf_op jit(solution)/shard_map/while/body/eval_jaxpr/hts,thd->shd/dot_general | solution.py:213
  342.2 7.2 %fusion.140 = bf16[2,64,512]{2,1,0:T(8,128)(2,1)S(1)} fusion(bf16[1024,2,64]{0,2,1:T(8,128)(2,1)S(1)} %bitcast.152, f32[2,512,1024]{2,1,0:T(8,128)} %subtract_exponential_fusion.3, f32[2,512,1024]{2,1,0:T(8,128)} %fusion.139), kind=kOutput, calls=%fused_computation.22.clone.1 | convolution fusion | flops 139462656 | bytes 8781824 | tf_op jit(solution)/shard_map/while/body/eval_jaxpr/hts,shd->thd/dot_general | solution.py:210
  359.5 7.3 %fusion.141 = bf16[2,64,1024]{2,1,0:T(8,128)(2,1)S(1)} fusion(bf16[512,2,64]{0,2,1:T(8,128)(2,1)S(1)} %bitcast.157, f32[2,512,1024]{2,1,0:T(8,128)} %subtract_exponential_fusion.3, f32[2,512,1024]{2,1,0:T(8,128)} %fusion.139), kind=kOutput, calls=%fused_computation.21.clone.1 | convolution fusion | flops 139462656 | bytes 8781824 | tf_op jit(solution)/shard_map/while/body/eval_jaxpr/hts,thd->shd/dot_general | solution.py:213
  371.1 7.9 %fusion.140 = bf16[2,64,512]{2,1,0:T(8,128)(2,1)S(1)} fusion(bf16[1024,2,64]{0,2,1:T(8,128)(2,1)S(1)} %bitcast.152, f32[2,512,1024]{2,1,0:T(8,128)} %subtract_exponential_fusion.3, f32[2,512,1024]{2,1,0:T(8,128)} %fusion.139), kind=kOutput, calls=%fused_computation.22.clone.1 | convolution fusion | flops 139462656 | bytes 8781824 | tf_op jit(solution)/shard_map/while/body/eval_jaxpr/hts,shd->thd/dot_general | solution.py:210
  389.1 7.1 %fusion.141 = bf16[2,64,1024]{2,1,0:T(8,128)(2,1)S(1)} fusion(bf16[512,2,64]{0,2,1:T(8,128)(2,1)S(1)} %bitcast.157, f32[2,512,1024]{2,1,0:T(8,128)} %subtract_exponential_fusion.3, f32[2,512,1024]{2,1,0:T(8,128)} %fusion.139), kind=kOutput, calls=%fused_computation.21.clone.1 | convolution fusion | flops 139462656 | bytes 8781824 | tf_op jit(solution)/shard_map/while/body/eval_jaxpr/hts,thd->shd/dot_general | solution.py:213
  400.4 7.2 %fusion.140 = bf16[2,64,512]{2,1,0:T(8,128)(2,1)S(1)} fusion(bf16[1024,2,64]{0,2,1:T(8,128)(2,1)S(1)} %bitcast.152, f32[2,512,1024]{2,1,0:T(8,128)} %subtract_exponential_fusion.3, f32[2,512,1024]{2,1,0:T(8,128)} %fusion.139), kind=kOutput, calls=%fused_computation.22.clone.1 | convolution fusion | flops 139462656 | bytes 8781824 | tf_op jit(solution)/shard_map/while/body/eval_jaxpr/hts,shd->thd/dot_general | solution.py:210
  417.7 7.1 %fusion.141 = bf16[2,64,1024]{2,1,0:T(8,128)(2,1)S(1)} fusion(bf16[512,2,64]{0,2,1:T(8,128)(2,1)S(1)} %bitcast.157, f32[2,512,1024]{2,1,0:T(8,128)} %subtract_exponential_fusion.3, f32[2,512,1024]{2,1,0:T(8,128)} %fusion.139), kind=kOutput, calls=%fused_computation.21.clone.1 | convolution fusion | flops 139462656 | bytes 8781824 | tf_op jit(solution)/shard_map/while/body/eval_jaxpr/hts,thd->shd/dot_general | solution.py:213
  429.0 7.2 %fusion.140 = bf16[2,64,512]{2,1,0:T(8,128)(2,1)S(1)} fusion(bf16[1024,2,64]{0,2,1:T(8,128)(2,1)S(1)} %bitcast.152, f32[2,512,1024]{2,1,0:T(8,128)} %subtract_exponential_fusion.3, f32[2,512,1024]{2,1,0:T(8,128)} %fusion.139), kind=kOutput, calls=%fused_computation.22.clone.1 | convolution fusion | flops 139462656 | bytes 8781824 | tf_op jit(solution)/shard_map/while/body/eval_jaxpr/hts,shd->thd/dot_general | solution.py:210
  446.2 7.8 %fusion.141 = bf16[2,64,1024]{2,1,0:T(8,128)(2,1)S(1)} fusion(bf16[512,2,64]{0,2,1:T(8,128)(2,1)S(1)} %bitcast.157, f32[2,512,1024]{2,1,0:T(8,128)} %subtract_exponential_fusion.3, f32[2,512,1024]{2,1,0:T(8,128)} %fusion.139), kind=kOutput, calls=%fused_computation.21.clone.1 | convolution fusion | flops 139462656 | bytes 8781824 | tf_op jit(solution)/shard_map/while/body/eval_jaxpr/hts,thd->shd/dot_general | solution.py:213
  458.3 7.2 %fusion.140 = bf16[2,64,512]{2,1,0:T(8,128)(2,1)S(1)} fusion(bf16[1024,2,64]{0,2,1:T(8,128)(2,1)S(1)} %bitcast.152, f32[2,512,1024]{2,1,0:T(8,128)} %subtract_exponential_fusion.3, f32[2,512,1024]{2,1,0:T(8,128)} %fusion.139), kind=kOutput, calls=%fused_computation.22.clone.1 | convolution fusion | flops 139462656 | bytes 8781824 | tf_op jit(solution)/shard_map/while/body/eval_jaxpr/hts,shd->thd/dot_general | solution.py:210
  475.6 7.1 %fusion.141 = bf16[2,64,1024]{2,1,0:T(8,128)(2,1)S(1)} fusion(bf16[512,2,64]{0,2,1:T(8,128)(2,1)S(1)} %bitcast.157, f32[2,512,1024]{2,1,0:T(8,128)} %subtract_exponential_fusion.3, f32[2,512,1024]{2,1,0:T(8,128)} %fusion.139), kind=kOutput, calls=%fused_computation.21.clone.1 | convolution fusion | flops 139462656 | bytes 8781824 | tf_op jit(solution)/shard_map/while/body/eval_jaxpr/hts,thd->shd/dot_general | solution.py:213
  487.0 7.2 %fusion.140 = bf16[2,64,512]{2,1,0:T(8,128)(2,1)S(1)} fusion(bf16[1024,2,64]{0,2,1:T(8,128)(2,1)S(1)} %bitcast.152, f32[2,512,1024]{2,1,0:T(8,128)} %subtract_exponential_fusion.3, f32[2,512,1024]{2,1,0:T(8,128)} %fusion.139), kind=kOutput, calls=%fused_computation.22.clone.1 | convolution fusion | flops 139462656 | bytes 8781824 | tf_op jit(solution)/shard_map/while/body/eval_jaxpr/hts,shd->thd/dot_general | solution.py:210
  495.0 17.0 %reduce-scatter.14.cloned.1.call-done = bf16[192,768]{1,0:T(8,128)(2,1)} async-done(((bf16[3072,768]{1,0:T(8,128)(2,1)}), bf16[192,768]{1,0:T(8,128)(2,1)}) %reduce-scatter.14.cloned.1.call-update) | async-done | bytes 294928 | tf_op jit(solution)/shard_map/reduce_scatter | solution.py:294
  512.0 44.9 %reduce-scatter.6.cloned.1.call-done = bf16[512,1536]{0,1:T(8,128)(2,1)} async-done(((bf16[1024,1536]{0,1:T(8,128)(2,1)}), bf16[512,1536]{0,1:T(8,128)(2,1)}) %reduce-scatter.6.cloned.1.call-update) | async-done | bytes 1572880 | tf_op jit(solution)/shard_map/reduce_scatter | solution.py:245
  556.9 5.6 convolution_convert_fusion.2
  567.4 5.0 fusion.68
  574.4 61.4 %all-reduce.18 = (bf16[768]{0:T(1024)(128)(2,1)S(1)}, bf16[768]{0:T(1024)(128)(2,1)S(1)}, bf16[768]{0:T(1024)(128)(2,1)S(1)}, bf16[768]{0:T(1024)(128)(2,1)S(1)}...) all-reduce(bf16[768]{0:T(1024)(128)(2,1)S(1)} %dynamic-update-slice, ...), channel_id=1, replica_groups=mesh['dp'=16,'ctx'=2] {'dp'}, use_global_device_ids=true, to_apply=%add.8 | all-reduce | flops 9984 | bytes 39936
  636.5 5.2 all-reduce.20
  649.4 9.0 %fusion.48 = bf16[1,512,768]{2,1,0:T(8,128)(2,1)} fusion(f32[512,768]{1,0:T(8,128)S(1)} %copy-done.5, bf16[3072,768]{1,0:T(8,128)(2,1)} %all-gather.15.cloned.1.call-done, f32[768]{0:T(1024)S(1)} %convert_element_type.218, f32[512,3072]{1,0:T(8,128)} %fusion.67, f32[3072]{0:T(1024)S(1)} %convert_element_type.216), kind=kOutput, calls=%fused_computation.82 | convolution fusion | flops 2432827392 | bytes 13384704 | tf_op jit(solution)/shard_map/dot_general | solution.py:162
  663.6 6.8 %all-gather = bf16[96,2304]{1,0:T(8,128)(2,1)S(1)} all-gather(bf16[48,2304]{1,0:T(8,128)(2,1)} %reduce-scatter.8.cloned.1.call-done), channel_id=2, replica_groups=mesh['dp'=16,'ctx'=2] {'ctx'}, dimensions={0}, use_global_device_ids=true | all-gather | bytes 663552 | tf_op jit(solution)/shard_map/all_gather | solution.py:319
  (291 shorter events, 201.2 us)
Async XLA Ops:
  7.2 76.3 %all-gather.7.cloned.1.call-start = ((), (), s32[]{:S(2)}) async-start(), calls=%async_computation.5 | async-start | bytes 3760128 | tf_op jit(solution)/shard_map/all_gather | solution.py:65
  7.9 123.8 %all-gather.9.cloned.1.call-start = ((), (), s32[]{:S(2)}) async-start(), calls=%async_computation.6 | async-start | bytes 4718592 | tf_op jit(solution)/shard_map/all_gather | solution.py:109
  83.5 4.5 copy-start.13
  88.0 3.8 copy-start.15
  88.0 5.1 copy-start.19
  88.0 6.4 copy-start.16
  88.0 6.4 copy-start.17
  88.0 6.4 copy-start.18
  89.3 103.7 %all-gather.11.cloned.1.call-start = ((), (), s32[]{:S(2)}) async-start(), calls=%async_computation.7 | async-start | bytes 1253376 | tf_op jit(solution)/shard_map/all_gather | solution.py:68
  90.0 136.5 %all-gather.13.cloned.1.call-start = ((), (), s32[]{:S(2)}) async-start(), calls=%async_computation.8 | async-start | bytes 5013504 | tf_op jit(solution)/shard_map/all_gather | solution.py:72
  90.6 189.8 %all-gather.15.cloned.1.call-start = ((), (), s32[]{:S(2)}) async-start(), calls=%async_computation.9 | async-start | bytes 5013504 | tf_op jit(solution)/shard_map/all_gather | solution.py:74
  91.2 403.7 %reduce-scatter.10.cloned.1.call-start = ((), (), s32[]{:S(2)}) async-start(), calls=%async_computation.12 | async-start | bytes 1253376 | tf_op jit(solution)/shard_map/reduce_scatter | solution.py:276
  136.5 57.3 %copy-start.1 = (bf16[1,512,768]{2,1,0:T(8,128)(2,1)S(1)}, bf16[1,512,768]{2,1,0:T(8,128)(2,1)}, u32[]{:S(2)}) copy-start(bf16[1,512,768]{2,1,0:T(8,128)(2,1)} %param.24) | copy-start | bytes 2359300
  148.5 1.9 copy-start
  157.8 1.9 copy-start
  167.2 1.9 copy-start
  186.1 1.9 copy-start
  192.9 3.4 copy-start.9
  196.0 93.7 %copy-start.4 = (f32[512,768]{1,0:T(8,128)}, f32[512,768]{1,0:T(8,128)S(1)}, u32[]{:S(2)}) copy-start(f32[512,768]{1,0:T(8,128)S(1)} %get-tuple-element.559) | copy-start | bytes 4718596
  196.3 84.0 %copy-start.2 = (bf16[1,512,768]{2,1,0:T(8,128)(2,1)S(1)}, bf16[1,512,768]{2,1,0:T(8,128)(2,1)}, u32[]{:S(2)}) copy-start(bf16[1,512,768]{2,1,0:T(8,128)(2,1)} %param.39) | copy-start | bytes 2359300
  280.4 9.4 %copy-start.20 = (bf16[768,3072]{1,0:T(8,128)(2,1)S(1)}, bf16[768,3072]{1,0:T(8,128)(2,1)}, u32[]{:S(2)}) copy-start(bf16[768,3072]{1,0:T(8,128)(2,1)} %all-gather.13.cloned.1.call-done) | copy-start | bytes 14155780
  289.7 3.0 copy-start.22
  292.7 3.3 copy-start.10
  297.9 197.1 %reduce-scatter.12.cloned.1.call-start = ((), (), s32[]{:S(2)}) async-start(), calls=%async_computation.13 | async-start | bytes 5013504 | tf_op jit(solution)/shard_map/reduce_scatter | solution.py:288
  305.4 206.6 %reduce-scatter.14.cloned.1.call-start = ((), (), s32[]{:S(2)}) async-start(), calls=%async_computation.14 | async-start | bytes 5013504 | tf_op jit(solution)/shard_map/reduce_scatter | solution.py:294
  314.1 242.8 %reduce-scatter.6.cloned.1.call-start = ((), (), s32[]{:S(2)}) async-start(), calls=%async_computation.10 | async-start | bytes 4718592 | tf_op jit(solution)/shard_map/reduce_scatter | solution.py:245
  494.8 62.1 %copy-start.8 = (bf16[512,768]{0,1:T(8,128)(2,1)S(1)}, bf16[512,768]{0,1:T(8,128)(2,1)}, u32[]{:S(2)}) copy-start(bf16[512,768]{0,1:T(8,128)(2,1)} %get-tuple-element.395) | copy-start | bytes 2359300
  494.9 163.5 %all-reduce.24.cloned.1.call-start = ((), (), s32[]{:S(2)}) async-start(), calls=%async_computation.15 | async-start | bytes 1327104 | tf_op jit(solution)/shard_map/psum | solution.py:322
  512.0 151.6 %reduce-scatter.8.cloned.1.call-start = ((), (), s32[]{:S(2)}) async-start(), calls=%async_computation.11 | async-start | bytes 3760128 | tf_op jit(solution)/shard_map/reduce_scatter | solution.py:267
  562.5 2.6 copy-start.21
  567.4 5.1 copy-start.14
  641.7 7.7 %copy-start.5 = (f32[512,768]{1,0:T(8,128)S(1)}, f32[512,768]{1,0:T(8,128)}, u32[]{:S(2)}) copy-start(f32[512,768]{1,0:T(8,128)} %copy-done.4) | copy-start | bytes 4718596
  (7 other events, 9.1 us)
Sparse Core Ops, SparseCore 0:
  10.3 50.2 all-gather.6
  89.4 42.2 all-gather.8
  134.0 38.2 all-gather.10
  174.5 51.9 all-gather.12
  228.7 51.6 all-gather.14
  298.0 56.7 reduce-scatter.9
  358.7 74.5 reduce-scatter.11
  437.1 74.8 reduce-scatter.13
  514.2 42.6 reduce-scatter.5
  559.2 31.7 all-reduce.23
  594.9 68.4 reduce-scatter.7
